TPU v7x, 32 devices: a whole 2x2x4 slice. The times are simulated.
32 devices in a mesh: expert: 16 (over z, y, x), dp: 2 (over core).
Axes of the slice: x: 2, y: 2, z: 4, core: 2. Of those that a mesh axis runs over, the one named last changes fastest.
Arguments:
- tokens: bfloat16 [8192, 4096], P('expert', 'dp'), may hold values from -6 to 6
- cotangent: bfloat16 [8192, 4096], P('expert', 'dp'), may hold values from -6 to 6
- routes: int32 [8192, 8], P('expert'), may hold values from 0 to 15, all different within a row; in each aligned block of 512 rows (0 to 511, 512 to 1023, ...) at most 512 rows name the same one
- probs: bfloat16 [8192, 8], P('expert'), may hold values from 0.099609375 to 1
- expert_slot: int32 [16], replicated, may hold values from 0 to 15, each once
- pull_flags: int32 [16], replicated, may hold values 0 or 1
- w_gate: bfloat16 [16, 768, 4096], P('expert', None, 'dp'), may hold values from -0.09375 to 0.09375
- w_up: bfloat16 [16, 768, 4096], P('expert', None, 'dp'), may hold values from -0.09375 to 0.09375
- w_down: bfloat16 [16, 768, 4096], P('expert', None, 'dp'), may hold values from -0.21875 to 0.21875
Outputs:
- expert_out: bfloat16 [8192, 4096], P('expert', 'dp')
- token_grad: bfloat16 [8192, 4096], P('expert', 'dp')
- gate_grad: bfloat16 [16, 768, 4096], P('expert', None, 'dp')
- up_grad: bfloat16 [16, 768, 4096], P('expert', None, 'dp')
- down_grad: bfloat16 [16, 768, 4096], P('expert', None, 'dp')
Inputs may be any that keep to these rules, and one draw needn't show every extreme that they name: `routes`: each row names 8 different experts. Within the 512 rows of one token batch no expert is named by more than 512 rows, and in some batch some expert is named by exactly 512 rows. `expert_slot`: A permutation of the experts.
All inputs are finite; a program needn't handle non-finite values.
Results may differ from a plain program's by a relative error of at most 0.006.
Values may be sent and summed in bfloat16 or wider, within the bound.
No kernel may reach another device: no remote copies, remote signals or barrier semaphores. Data moves between devices by JAX's collectives and lax.ppermute only.
A program may use at most 128 MiB of HBM per device.

v0:
```python
import jax
import jax.numpy as jnp
from jax import lax
from jax.sharding import PartitionSpec as P


def passed_along(value, axis, steps):
    count = lax.axis_size(axis)
    pairs = [(source, (source + steps) % count) for source in range(count)]
    return lax.ppermute(value, axis, pairs)


def silu_parts(gate_val):
    sigmoid_val = jax.nn.sigmoid(gate_val)
    return (gate_val * sigmoid_val, sigmoid_val * (1.0 + gate_val * (1.0 - sigmoid_val)))


def slot_rows(route_ids, weights_in, expert, scale, capacity):
    count = route_ids.shape[0]
    hit = route_ids == expert
    member = jnp.any(hit, axis=1)
    weight = jnp.sum(jnp.where(hit, weights_in.astype(jnp.float32), 0.0), axis=1) * scale
    rank = jnp.cumsum(member.astype(jnp.int32), dtype=jnp.int32) - 1
    entries = jnp.arange(capacity, dtype=jnp.int32)
    chosen = member[None, :] & (rank[None, :] == entries[:, None])
    positions = jnp.arange(count, dtype=jnp.int32)
    index = jnp.sum(jnp.where(chosen, positions[None, :], 0), axis=1, dtype=jnp.int32)
    index = jnp.where(jnp.any(chosen, axis=1), index, count)
    return (index, jnp.take(weight, index, mode="fill", fill_value=0.0))


def hidden_values(gate_val, up_val, back_val, rows_w):
    activated, slope_val = silu_parts(gate_val)
    weight_col = rows_w[..., None]
    scaled = (weight_col * activated * up_val).astype(jnp.bfloat16)
    grad_gate = (back_val * weight_col * up_val * slope_val).astype(jnp.bfloat16)
    grad_up = (back_val * weight_col * activated).astype(jnp.bfloat16)
    return (scaled, grad_gate, grad_up)


def take_rows(array, index):
    return jnp.take(array, index, axis=0, mode="fill", fill_value=0)


def finish_set(scaled, grad_gate, grad_up, rows_x, rows_dy, wg, wu, wd):
    out_rows = jnp.dot(scaled, wd, preferred_element_type=jnp.float32)
    in_rows = jnp.dot(grad_gate, wg, preferred_element_type=jnp.float32)
    in_rows = in_rows + jnp.dot(grad_up, wu, preferred_element_type=jnp.float32)
    over_rows = (((0,), (0,)), ((), ()))
    grad_terms = (
        lax.dot_general(grad_gate, rows_x, over_rows, preferred_element_type=jnp.float32),
        lax.dot_general(grad_up, rows_x, over_rows, preferred_element_type=jnp.float32),
        lax.dot_general(scaled, rows_dy, over_rows, preferred_element_type=jnp.float32),
    )
    return (out_rows, in_rows, tuple((term.astype(jnp.bfloat16) for term in grad_terms)))


def per_device(tokens, cotangent, routes, probs, expert_slot, pull_flags, w_gate, w_up, w_down):
    columns = lax.axis_size("expert")
    column = lax.axis_index("expert")
    count = tokens.shape[0]
    capacity = min(count, count * routes.shape[1] * 2 // columns)
    labels = jnp.arange(columns, dtype=jnp.int32)
    following = (column + 1) % columns

    def owner_expert(slot):
        return jnp.sum(jnp.where(expert_slot == slot, labels, 0), dtype=jnp.int32)

    flag = pull_flags[column].astype(jnp.float32)
    own_index, own_weight = slot_rows(routes, probs, owner_expert(column), 1.0, capacity)
    next_index, next_weight = slot_rows(routes, probs, owner_expert(following), flag, capacity)
    own_x = take_rows(tokens, own_index)
    own_dy = take_rows(cotangent, own_index)
    next_x = take_rows(tokens, next_index)
    next_dy = take_rows(cotangent, next_index)
    own_set = (own_x, own_dy, own_weight, w_gate[0], w_up[0], w_down[0])
    arrived = passed_along((next_x, next_dy, next_weight.astype(jnp.bfloat16)), "expert", 1)
    far_set = (
        arrived[0],
        arrived[1],
        arrived[2].astype(jnp.float32),
        w_gate[0],
        w_up[0],
        w_down[0],
    )
    both_sets = (own_set, far_set)
    contract = (((1,), (1,)), ((), ()))
    partial_gate = jnp.stack(
        [
            lax.dot_general(one[0], one[3], contract, preferred_element_type=jnp.float32)
            for one in both_sets
        ]
    )
    partial_up = jnp.stack(
        [
            lax.dot_general(one[0], one[4], contract, preferred_element_type=jnp.float32)
            for one in both_sets
        ]
    )
    partial_back = jnp.stack(
        [
            lax.dot_general(one[1], one[5], contract, preferred_element_type=jnp.float32)
            for one in both_sets
        ]
    )
    gate_val, up_val, back_val = (
        lax.psum_scatter(partial_gate, "dp", scatter_dimension=2, tiled=True),
        lax.psum_scatter(partial_up, "dp", scatter_dimension=2, tiled=True),
        lax.psum_scatter(partial_back, "dp", scatter_dimension=2, tiled=True),
    )
    rows_w = jnp.stack([own_set[2], far_set[2]])
    scaled, grad_gate, grad_up = hidden_values(gate_val, up_val, back_val, rows_w)
    scaled, grad_gate, grad_up = (
        lax.all_gather(scaled, "dp", axis=2, tiled=True),
        lax.all_gather(grad_gate, "dp", axis=2, tiled=True),
        lax.all_gather(grad_up, "dp", axis=2, tiled=True),
    )
    own_out, own_in, own_grads = finish_set(
        scaled[0],
        grad_gate[0],
        grad_up[0],
        own_set[0],
        own_set[1],
        own_set[3],
        own_set[4],
        own_set[5],
    )
    far_out, far_in, far_grads = finish_set(
        scaled[1],
        grad_gate[1],
        grad_up[1],
        far_set[0],
        far_set[1],
        far_set[3],
        far_set[4],
        far_set[5],
    )
    next_out, next_in = (
        passed_along(far_out.astype(jnp.bfloat16), "expert", -1).astype(far_out.dtype),
        passed_along(far_in.astype(jnp.bfloat16), "expert", -1).astype(far_in.dtype),
    )
    grad_sums = tuple(
        (
            (
                lax.optimization_barrier(mine).astype(jnp.float32)
                + lax.optimization_barrier(theirs).astype(jnp.float32)
            ).astype(jnp.bfloat16)
            for mine, theirs in zip(own_grads, far_grads)
        )
    )
    empty = jnp.zeros(tokens.shape, jnp.float32)
    out_part = (
        empty.at[own_index].add(own_out, mode="drop").at[next_index].add(next_out, mode="drop")
    )
    in_part = empty.at[own_index].add(own_in, mode="drop").at[next_index].add(next_in, mode="drop")
    return (
        out_part.astype(jnp.bfloat16),
        in_part.astype(jnp.bfloat16),
        grad_sums[0][None],
        grad_sums[1][None],
        grad_sums[2][None],
    )


def solution(mesh):
    return jax.shard_map(
        per_device,
        mesh=mesh,
        in_specs=(
            P("expert", "dp"),
            P("expert", "dp"),
            P("expert", None),
            P("expert", None),
            P(),
            P(),
            P("expert", None, "dp"),
            P("expert", None, "dp"),
            P("expert", None, "dp"),
        ),
        out_specs=(
            P("expert", "dp"),
            P("expert", "dp"),
            P("expert", None, "dp"),
            P("expert", None, "dp"),
            P("expert", None, "dp"),
        ),
        check_vma=False,
    )
```

profile of v0, /device:TPU:0, one launch (start us, length us, event | category | flops | bytes accessed | tf_op | source)
XLA Modules:
  0.0 333.3 jit_solution(14110842430651859816)
XLA Ops:
  11.9 7.1 %gather_fusion.5 = bf16[512,2048]{1,0:T(8,128)(2,1)} fusion(bf16[512,2048]{1,0:T(8,128)(2,1)} %param.14, s32[1024]{0:T(1024)S(1)} %pad_clamp_fusion), kind=kCustom, calls=%fused_computation.5.clone | custom fusion | bytes 4196352 | tf_op jit(solution)/shard_map/jit(_take)/gather | solution.py:42
  19.0 7.1 %gather_fusion.3 = bf16[512,2048]{1,0:T(8,128)(2,1)} fusion(bf16[512,2048]{1,0:T(8,128)(2,1)} %param.13, s32[1024]{0:T(1024)S(1)} %pad_clamp_fusion), kind=kCustom, calls=%fused_computation.3.clone | custom fusion | bytes 4196352 | tf_op jit(solution)/shard_map/jit(_take)/gather | solution.py:42
  30.9 4.6 %broadcast_select_fusion = (bf16[512,2048]{1,0:T(8,128)(2,1)}, bf16[512,2048]{1,0:T(8,128)(2,1)}) fusion(bf16[512,2048]{1,0:T(8,128)(2,1)} %gather_fusion.5, pred[512]{0:T(512)(128)(4,1)S(1)} %get-tuple-element.14, bf16[512,2048]{1,0:T(8,128)(2,1)} %gather_fusion.3), kind=kLoop, calls=%fused_computation.60 | loop fusion | flops 2097152 | bytes 8389120 | tf_op jit(solution)/shard_map/jit(_take)/select_n | solution.py:42
  40.1 7.1 %gather_fusion.2 = bf16[512,2048]{1,0:T(8,128)(2,1)} fusion(bf16[512,2048]{1,0:T(8,128)(2,1)} %param.13, s32[1024]{0:T(1024)S(1)} %pad_clamp_fusion.1), kind=kCustom, calls=%fused_computation.1.clone | custom fusion | bytes 4196352 | tf_op jit(solution)/shard_map/jit(_take)/gather | solution.py:42
  50.8 4.5 %fusion.42 = f32[1,512,768]{2,1,0:T(8,128)S(1)} fusion(bf16[1,768,2048]{2,1,0:T(8,128)(2,1)} %param.19, bf16[512,2048]{1,0:T(8,128)(2,1)} %gather_fusion.2, pred[512]{0:T(512)(128)(4,1)S(1)} %get-tuple-element.12), kind=kOutput, calls=%fused_computation.69 | convolution fusion | flops 1611661312 | bytes 6816256 | tf_op jit(solution)/shard_map/dot_general | solution.py:90
  55.3 33.6 %collective-permute-done.1 = bf16[512,2048]{1,0:T(8,128)(2,1)} collective-permute-done((bf16[512,2048]{1,0:T(8,128)(2,1)}, bf16[512,2048]{1,0:T(8,128)(2,1)}, u32[]{:S(2)}, u32[]{:S(2)}) %collective-permute-start.1) | collective-permute-done | bytes 2097184 | tf_op jit(solution)/shard_map/ppermute | solution.py:10
  103.5 7.1 %gather_fusion.4 = bf16[512,2048]{1,0:T(8,128)(2,1)} fusion(bf16[512,2048]{1,0:T(8,128)(2,1)} %param.14, s32[1024]{0:T(1024)S(1)} %pad_clamp_fusion.1), kind=kCustom, calls=%fused_computation.4.clone | custom fusion | bytes 4196352 | tf_op jit(solution)/shard_map/jit(_take)/gather | solution.py:42
  110.6 4.9 %fusion.54 = f32[1,512,768]{2,1,0:T(8,128)S(1)} fusion(bf16[1,768,2048]{2,1,0:T(8,128)(2,1)} %param.21, bf16[512,2048]{1,0:T(8,128)(2,1)} %gather_fusion.4, pred[512]{0:T(512)(128)(4,1)S(1)} %get-tuple-element.12), kind=kOutput, calls=%fused_computation.73 | convolution fusion | flops 1611661312 | bytes 6816256 | tf_op jit(solution)/shard_map/dot_general | solution.py:102
  115.5 39.0 %collective-permute-done.3 = bf16[512,2048]{1,0:T(8,128)(2,1)} collective-permute-done((bf16[512,2048]{1,0:T(8,128)(2,1)}, bf16[512,2048]{1,0:T(8,128)(2,1)}, u32[]{:S(2)}, u32[]{:S(2)}) %collective-permute-start.3) | collective-permute-done | bytes 2097184 | tf_op jit(solution)/shard_map/ppermute | solution.py:10
  159.9 7.2 %collective-permute-done = bf16[512]{0:T(512)(128)(2,1)S(1)} collective-permute-done((bf16[512]{0:T(512)(128)(2,1)S(1)}, bf16[512]{0:T(512)(128)(2,1)S(1)}, u32[]{:S(2)}, u32[]{:S(2)}) %collective-permute-start) | collective-permute-done | bytes 1056 | tf_op jit(solution)/shard_map/ppermute | solution.py:10
  167.2 4.7 %multiply_convert_fusion = (bf16[2,512,384]{2,1,0:T(8,128)(2,1)}, bf16[2,512,384]{2,1,0:T(8,128)(2,1)}, bf16[2,512,384]{2,1,0:T(8,128)(2,1)}) fusion(f32[2,512,384]{2,1,0:T(8,128)} %reduce-scatter.8.cloned.1.call-done, f32[2,512]{1,0:T(2,128)S(1)} %pad_maximum_fusion.3, f32[2,512,384]{2,1,0:T(8,128)} %reduce-scatter.4.cloned.1.call-done, ...), kind=kLoop, calls=%fused_computation.64 | loop fusion | flops 6684672 | bytes 7081984 | tf_op jit(solution)/shard_map/convert_element_type | solution.py:37
  173.1 9.6 %all-gather.8.cloned.1.call-done = bf16[2,512,768]{2,1,0:T(8,128)(2,1)} async-done(((bf16[2,512,384]{2,1,0:T(8,128)(2,1)}), bf16[2,512,768]{2,1,0:T(8,128)(2,1)}) %all-gather.8.cloned.1.call-update) | async-done | bytes 1572880 | tf_op jit(solution)/shard_map/all_gather | solution.py:116
  182.7 4.9 %fusion.17 = f32[512,2048]{1,0:T(8,128)} fusion(bf16[1,768,2048]{2,1,0:T(8,128)(2,1)S(1)} %copy-done, bf16[2,512,768]{2,1,0:T(8,128)(2,1)} %all-gather.8.cloned.1.call-done), kind=kOutput, calls=%fused_computation.40 | convolution fusion | flops 1610612736 | bytes 8126464 | tf_op jit(solution)/shard_map/dot_general | solution.py:48
  187.5 8.1 %all-gather.6.cloned.1.call-done = bf16[2,512,768]{2,1,0:T(8,128)(2,1)} async-done(((bf16[2,512,384]{2,1,0:T(8,128)(2,1)}), bf16[2,512,768]{2,1,0:T(8,128)(2,1)}) %all-gather.6.cloned.1.call-update) | async-done | bytes 1572880 | tf_op jit(solution)/shard_map/all_gather | solution.py:115
  195.6 6.5 %add_convert_fusion.3 = bf16[512,2048]{1,0:T(8,128)(2,1)} fusion(f32[512,2048]{1,0:T(8,128)} %fusion.17, bf16[1,768,2048]{2,1,0:T(8,128)(2,1)} %param.19, bf16[2,512,768]{2,1,0:T(8,128)(2,1)} %all-gather.6.cloned.1.call-done), kind=kOutput, calls=%fused_computation.15 | convolution fusion | flops 1612709888 | bytes 10223616 | tf_op jit(solution)/shard_map/dot_general | solution.py:47
  202.1 5.4 %collective-permute-start.4 = (bf16[512,2048]{1,0:T(8,128)(2,1)}, bf16[512,2048]{1,0:T(8,128)(2,1)}, u32[]{:S(2)}, u32[]{:S(2)}) collective-permute-start(bf16[512,2048]{1,0:T(8,128)(2,1)} %add_convert_fusion.3), channel_id=1, source_target_pairs={{0,30},{2,0},{4,2},{6,4},{8,6},{10,8},{12,10},{14,12},{16,14},{18,... | collective-permute-start | bytes 6291464 | tf_op jit(solution)/shard_map/ppermute | solution.py:10
  208.5 5.3 %fusion.33 = bf16[512,2048]{1,0:T(8,128)(2,1)} fusion(bf16[1,768,2048]{2,1,0:T(8,128)(2,1)} %param.21, bf16[2,512,768]{2,1,0:T(8,128)(2,1)} %all-gather.4.cloned.1.call-done), kind=kOutput, calls=%fused_computation.56 | convolution fusion | flops 1611661312 | bytes 6029312 | tf_op jit(solution)/shard_map/dot_general | solution.py:46
  213.9 5.6 %collective-permute-start.2 = (bf16[512,2048]{1,0:T(8,128)(2,1)}, bf16[512,2048]{1,0:T(8,128)(2,1)}, u32[]{:S(2)}, u32[]{:S(2)}) collective-permute-start(bf16[512,2048]{1,0:T(8,128)(2,1)} %fusion.33), channel_id=1, source_target_pairs={{0,30},{2,0},{4,2},{6,4},{8,6},{10,8},{12,10},{14,12},{16,14},{18,... | collective-permute-start | bytes 6291464 | tf_op jit(solution)/shard_map/ppermute | solution.py:10
  219.5 5.1 %convolution_convert_fusion.2 = bf16[768,2048]{1,0:T(8,128)(2,1)} fusion(bf16[512,2048]{1,0:T(8,128)(2,1)} %collective-permute-done.1, bf16[2,512,768]{2,1,0:T(8,128)(2,1)S(1)} %copy-done.11), kind=kOutput, calls=%fused_computation.22 | convolution fusion | flops 1612185600 | bytes 6029312 | tf_op jit(solution)/shard_map/dot_general | solution.py:52
  228.1 5.2 %convolution_convert_fusion = bf16[768,2048]{1,0:T(8,128)(2,1)} fusion(bf16[512,2048]{1,0:T(8,128)(2,1)} %collective-permute-done.3, bf16[2,512,768]{2,1,0:T(8,128)(2,1)S(1)} %copy-done.13), kind=kOutput, calls=%fused_computation.20 | convolution fusion | flops 1612185600 | bytes 6029312 | tf_op jit(solution)/shard_map/dot_general | solution.py:53
  233.4 3.6 %convolution_convert_fusion.1 = bf16[768,2048]{1,0:T(8,128)(2,1)} fusion(bf16[512,2048]{1,0:T(8,128)(2,1)S(1)} %copy-done.6, pred[512]{0:T(512)(128)(4,1)S(1)} %get-tuple-element.12, bf16[2,512,768]{2,1,0:T(8,128)(2,1)S(1)} %copy-done.13), kind=kOutput, calls=%fused_computation.21 | convolution fusion | flops 1613234176 | bytes 6029824 | tf_op jit(solution)/shard_map/dot_general | solution.py:53
  240.6 3.8 %fusion.19 = f32[512,2048]{1,0:T(8,128)} fusion(bf16[1,768,2048]{2,1,0:T(8,128)(2,1)S(1)} %copy-done, bf16[2,512,768]{2,1,0:T(8,128)(2,1)S(1)} %copy-done.11), kind=kOutput, calls=%fused_computation.42 | convolution fusion | flops 1610612736 | bytes 8126464 | tf_op jit(solution)/shard_map/dot_general | solution.py:48
  244.4 3.8 %fusion.27 = f32[512,2048]{1,0:T(8,128)} fusion(bf16[1,768,2048]{2,1,0:T(8,128)(2,1)S(1)} %copy-done.8, bf16[2,512,768]{2,1,0:T(8,128)(2,1)S(1)} %copy-done.12), kind=kOutput, calls=%fused_computation.50 | convolution fusion | flops 1610612736 | bytes 8126464 | tf_op jit(solution)/shard_map/dot_general | solution.py:47
  248.2 3.8 %fusion.15 = f32[512,2048]{1,0:T(8,128)} fusion(bf16[1,768,2048]{2,1,0:T(8,128)(2,1)S(1)} %copy-done.10, bf16[2,512,768]{2,1,0:T(8,128)(2,1)S(1)} %copy-done.13), kind=kOutput, calls=%fused_computation.38 | convolution fusion | flops 1610612736 | bytes 8126464 | tf_op jit(solution)/shard_map/dot_general | solution.py:46
  251.9 5.5 %convolution_convert_fusion.4 = bf16[768,2048]{1,0:T(8,128)(2,1)} fusion(bf16[512,2048]{1,0:T(8,128)(2,1)} %collective-permute-done.1, bf16[2,512,768]{2,1,0:T(8,128)(2,1)S(1)} %copy-done.12), kind=kOutput, calls=%fused_computation.24 | convolution fusion | flops 1612185600 | bytes 6029312 | tf_op jit(solution)/shard_map/dot_general | solution.py:51
  257.5 10.7 %scatter_custom_fusion = f32[512,2048]{1,0:T(8,128)} fusion(s32[512]{0:T(512)S(1)} %bitcast.112, f32[512,2048]{1,0:T(8,128)} %fusion.15, f32[]{:T(128)} %constant.31.clone.1), kind=kCustom, calls=%fused_computation.58 | custom fusion | flops 1048576 | bytes 4194816 | tf_op jit(solution)/shard_map/scatter-add | solution.py:153
  268.2 12.5 %scatter_custom_fusion.2 = f32[512,2048]{1,0:T(8,128)} fusion(s32[512]{0:T(512)S(1)} %bitcast.113, f32[512,2048]{1,0:T(8,128)} %fusion.27, f32[512,2048]{1,0:T(8,128)} %fusion.19, f32[]{:T(128)} %constant.31.clone.1), kind=kCustom, calls=%fused_computation.16 | custom fusion | flops 2097152 | bytes 12582916 | tf_op jit(solution)/shard_map/scatter-add | solution.py:155
  280.8 6.2 %fusion.7 = bf16[1,768,2048]{2,1,0:T(8,128)(2,1)} fusion(bf16[768,2048]{1,0:T(8,128)(2,1)} %convolution_convert_fusion.2, bf16[768,2048]{1,0:T(8,128)(2,1)} %convolution_convert_fusion.3), kind=kLoop, calls=%fused_computation.27 | loop fusion | flops 6291456 | bytes 9437184 | tf_op jit(solution)/shard_map/broadcast_in_dim | solution.py:160
  293.9 12.4 %scatter_custom_fusion.3 = f32[512,2048]{1,0:T(8,128)} fusion(f32[512,2048]{1,0:T(8,128)} %scatter_custom_fusion.2, s32[512]{0:T(512)S(1)} %bitcast.110, bf16[512,2048]{1,0:T(8,128)(2,1)} %collective-permute-done.4), kind=kCustom, calls=%fused_computation.13 | custom fusion | flops 2097152 | bytes 6291456 | tf_op jit(solution)/shard_map/scatter-add | solution.py:155
  306.4 3.8 %convert_element_type.116 = bf16[512,2048]{1,0:T(8,128)(2,1)} convert(f32[512,2048]{1,0:T(8,128)} %scatter_custom_fusion.3) | non-fusion elementwise | flops 1048576 | bytes 6291456 | tf_op jit(solution)/shard_map/convert_element_type | solution.py:158
  310.2 12.2 %scatter_custom_fusion.1 = f32[512,2048]{1,0:T(8,128)} fusion(f32[512,2048]{1,0:T(8,128)} %scatter_custom_fusion, s32[512]{0:T(512)S(1)} %bitcast.111, bf16[512,2048]{1,0:T(8,128)(2,1)} %collective-permute-done.2), kind=kCustom, calls=%fused_computation.18 | custom fusion | flops 2097152 | bytes 6291456 | tf_op jit(solution)/shard_map/scatter-add | solution.py:153
  322.4 3.8 %convert_element_type.111 = bf16[512,2048]{1,0:T(8,128)(2,1)} convert(f32[512,2048]{1,0:T(8,128)} %scatter_custom_fusion.1) | non-fusion elementwise | flops 1048576 | bytes 6291456 | tf_op jit(solution)/shard_map/convert_element_type | solution.py:157
  (96 shorter events, 53.2 us)
Async XLA Ops:
  7.2 87.1 %copy-start = (bf16[1,768,2048]{2,1,0:T(8,128)(2,1)S(1)}, bf16[1,768,2048]{2,1,0:T(8,128)(2,1)}, u32[]{:S(2)}) copy-start(bf16[1,768,2048]{2,1,0:T(8,128)(2,1)} %param.20) | copy-start | bytes 9437188
  7.2 159.9 %reduce-scatter.4.cloned.1.call-start = ((), (), s32[]{:S(2)}) async-start(), calls=%async_computation.3 | async-start | bytes 4718592 | tf_op jit(solution)/shard_map/reduce_scatter | solution.py:107
  19.0 7.1 %copy-start.14 = (s32[16]{0:T(128)S(1)}, s32[16]{0:T(128)}, u32[]{:S(2)}) copy-start(s32[16]{0:T(128)} %param.18) | copy-start | bytes 196
  35.5 53.4 %collective-permute-start.1 = (bf16[512,2048]{1,0:T(8,128)(2,1)}, bf16[512,2048]{1,0:T(8,128)(2,1)}, u32[]{:S(2)}, u32[]{:S(2)}) collective-permute-start(bf16[512,2048]{1,0:T(8,128)(2,1)} %get-tuple-element.25), channel_id=1, source_target_pairs={{0,2},{2,4},{4,6},{6,8},{8,10},{10,12},{12,14},{14,16},{16,18},{18... | collective-permute-start | bytes 6291464 | tf_op jit(solution)/shard_map/ppermute | solution.py:10
  50.8 38.1 %copy-start.7 = (bf16[1,768,2048]{2,1,0:T(8,128)(2,1)S(1)}, bf16[1,768,2048]{2,1,0:T(8,128)(2,1)}, u32[]{:S(2)}) copy-start(bf16[1,768,2048]{2,1,0:T(8,128)(2,1)} %param.19) | copy-start | bytes 9437188
  94.2 72.9 %reduce-scatter.6.cloned.1.call-start = ((), (), s32[]{:S(2)}) async-start(), calls=%async_computation.4 | async-start | bytes 4718592 | tf_op jit(solution)/shard_map/reduce_scatter | solution.py:108
  103.2 64.0 %reduce-scatter.8.cloned.1.call-start = ((), (), s32[]{:S(2)}) async-start(), calls=%async_computation.6 | async-start | bytes 4718592 | tf_op jit(solution)/shard_map/reduce_scatter | solution.py:109
  103.3 51.2 %collective-permute-start.3 = (bf16[512,2048]{1,0:T(8,128)(2,1)}, bf16[512,2048]{1,0:T(8,128)(2,1)}, u32[]{:S(2)}, u32[]{:S(2)}) collective-permute-start(bf16[512,2048]{1,0:T(8,128)(2,1)} %get-tuple-element.24), channel_id=1, source_target_pairs={{0,2},{2,4},{4,6},{6,8},{8,10},{10,12},{12,14},{14,16},{16,18},{18... | collective-permute-start | bytes 6291464 | tf_op jit(solution)/shard_map/ppermute | solution.py:10
  110.6 43.9 %copy-start.9 = (bf16[1,768,2048]{2,1,0:T(8,128)(2,1)S(1)}, bf16[1,768,2048]{2,1,0:T(8,128)(2,1)}, u32[]{:S(2)}) copy-start(bf16[1,768,2048]{2,1,0:T(8,128)(2,1)} %param.21) | copy-start | bytes 9437188
  159.8 22.9 %all-gather.8.cloned.1.call-start = ((), (), s32[]{:S(2)}) async-start(), calls=%async_computation.8 | async-start | bytes 2359296 | tf_op jit(solution)/shard_map/all_gather | solution.py:116
  159.9 7.2 %collective-permute-start = (bf16[512]{0:T(512)(128)(2,1)S(1)}, bf16[512]{0:T(512)(128)(2,1)S(1)}, u32[]{:S(2)}, u32[]{:S(2)}) collective-permute-start(bf16[512]{0:T(512)(128)(2,1)S(1)} %get-tuple-element.13), channel_id=1, source_target_pairs={{0,2},{2,4},{4,6},{6,8},{8,10},{10,12},{12,14},{14,16},{16,18},{18... | collective-permute-start | bytes 3080 | tf_op jit(solution)/shard_map/ppermute | solution.py:10
  171.9 23.7 %all-gather.6.cloned.1.call-start = ((), (), s32[]{:S(2)}) async-start(), calls=%async_computation.7 | async-start | bytes 2359296 | tf_op jit(solution)/shard_map/all_gather | solution.py:115
  172.5 36.1 %all-gather.4.cloned.1.call-start = ((), (), s32[]{:S(2)}) async-start(), calls=%async_computation.5 | async-start | bytes 2359296 | tf_op jit(solution)/shard_map/all_gather | solution.py:114
  202.1 91.8 %collective-permute-start.4 = (bf16[512,2048]{1,0:T(8,128)(2,1)}, bf16[512,2048]{1,0:T(8,128)(2,1)}, u32[]{:S(2)}, u32[]{:S(2)}) collective-permute-start(bf16[512,2048]{1,0:T(8,128)(2,1)} %add_convert_fusion.3), channel_id=1, source_target_pairs={{0,30},{2,0},{4,2},{6,4},{8,6},{10,8},{12,10},{14,12},{16,14},{18,... | collective-permute-start | bytes 6291464 | tf_op jit(solution)/shard_map/ppermute | solution.py:10
  208.5 10.9 %copy-start.11 = (bf16[2,512,768]{2,1,0:T(8,128)(2,1)S(1)}, bf16[2,512,768]{2,1,0:T(8,128)(2,1)}, u32[]{:S(2)}) copy-start(bf16[2,512,768]{2,1,0:T(8,128)(2,1)} %all-gather.8.cloned.1.call-done) | copy-start | bytes 4718596
  213.9 10.7 %copy-start.5 = (bf16[512,2048]{1,0:T(8,128)(2,1)S(1)}, bf16[512,2048]{1,0:T(8,128)(2,1)}, u32[]{:S(2)}) copy-start(bf16[512,2048]{1,0:T(8,128)(2,1)} %gather_fusion.2) | copy-start | bytes 6291460
  213.9 96.3 %collective-permute-start.2 = (bf16[512,2048]{1,0:T(8,128)(2,1)}, bf16[512,2048]{1,0:T(8,128)(2,1)}, u32[]{:S(2)}, u32[]{:S(2)}) collective-permute-start(bf16[512,2048]{1,0:T(8,128)(2,1)} %fusion.33), channel_id=1, source_target_pairs={{0,30},{2,0},{4,2},{6,4},{8,6},{10,8},{12,10},{14,12},{16,14},{18,... | collective-permute-start | bytes 6291464 | tf_op jit(solution)/shard_map/ppermute | solution.py:10
  224.6 3.6 %copy-start.13 = (bf16[2,512,768]{2,1,0:T(8,128)(2,1)S(1)}, bf16[2,512,768]{2,1,0:T(8,128)(2,1)}, u32[]{:S(2)}) copy-start(bf16[2,512,768]{2,1,0:T(8,128)(2,1)} %all-gather.4.cloned.1.call-done) | copy-start | bytes 4718596
  228.1 5.2 %copy-start.6 = (bf16[512,2048]{1,0:T(8,128)(2,1)S(1)}, bf16[512,2048]{1,0:T(8,128)(2,1)}, u32[]{:S(2)}) copy-start(bf16[512,2048]{1,0:T(8,128)(2,1)} %gather_fusion.4) | copy-start | bytes 6291460
  233.4 3.6 %copy-start.12 = (bf16[2,512,768]{2,1,0:T(8,128)(2,1)S(1)}, bf16[2,512,768]{2,1,0:T(8,128)(2,1)}, u32[]{:S(2)}) copy-start(bf16[2,512,768]{2,1,0:T(8,128)(2,1)} %all-gather.6.cloned.1.call-done) | copy-start | bytes 4718596
  240.6 3.8 %copy-start.8 = (bf16[1,768,2048]{2,1,0:T(8,128)(2,1)S(1)}, bf16[1,768,2048]{2,1,0:T(8,128)(2,1)}, u32[]{:S(2)}) copy-start(bf16[1,768,2048]{2,1,0:T(8,128)(2,1)} %param.19) | copy-start | bytes 9437188
  244.4 3.8 %copy-start.10 = (bf16[1,768,2048]{2,1,0:T(8,128)(2,1)S(1)}, bf16[1,768,2048]{2,1,0:T(8,128)(2,1)}, u32[]{:S(2)}) copy-start(bf16[1,768,2048]{2,1,0:T(8,128)(2,1)} %param.21) | copy-start | bytes 9437188
  280.7 6.3 %copy-start.1 = (bf16[768,2048]{1,0:T(8,128)(2,1)S(1)}, bf16[768,2048]{1,0:T(8,128)(2,1)}, u32[]{:S(2)}) copy-start(bf16[768,2048]{1,0:T(8,128)(2,1)} %convolution_convert_fusion) | copy-start | bytes 9437188
  280.7 6.3 %copy-start.2 = (bf16[768,2048]{1,0:T(8,128)(2,1)S(1)}, bf16[768,2048]{1,0:T(8,128)(2,1)}, u32[]{:S(2)}) copy-start(bf16[768,2048]{1,0:T(8,128)(2,1)} %convolution_convert_fusion.1) | copy-start | bytes 9437188
  287.0 3.1 copy-start.3
  287.0 3.8 %copy-start.4 = (bf16[768,2048]{1,0:T(8,128)(2,1)S(1)}, bf16[768,2048]{1,0:T(8,128)(2,1)}, u32[]{:S(2)}) copy-start(bf16[768,2048]{1,0:T(8,128)(2,1)} %convolution_convert_fusion.4) | copy-start | bytes 9437188
Sparse Core Ops, SparseCore 0:
  94.3 8.4 reduce-scatter.3
  105.6 12.2 reduce-scatter.5
  159.9 6.8 reduce-scatter.7
  172.0 10.6 all-gather.7
  184.6 10.9 all-gather.5
  197.6 10.9 all-gather.3
where the time goes:
time: 339 us; the launch traced here: 333 us
  waiting for transfers between devices  99.6 us (29%)
  other arithmetic  88.3 us (26%)
  matrix products  78 us (23%)
  local copies, waits for them, and re-layouts  37.1 us (11%)
  between operations  15.3 us (5%)
  starting transfers between devices  15 us (4%)
    ppermute x5, waiting for transfers between devices, passed_along(): return lax.ppermute(value, axis, pairs)  79.7 us
    gather x4, local copies, waits for them, and re-layouts, take_rows(): return jnp.take(array, index, axis=0, mode='fill', fill_value=0)  28.4 us
    scatter-add x2, other arithmetic, per_device(): empty.at[own_index].add(own_in, mode='drop').at[next_index]  25 us
    scatter-add x2, other arithmetic, per_device(): empty.at[own_index].add(own_out, mode='drop').at[next_index]  22.9 us
    ppermute x5, starting transfers between devices, passed_along(): return lax.ppermute(value, axis, pairs)  14.8 us
    dot_general x2, matrix products, finish_set(): in_rows = jnp.dot(grad_gate, wg, preferred_element_type=jnp.float32)  10.3 us
    all_gather x1, waiting for transfers between devices, per_device(): lax.all_gather(grad_up, 'dp', axis=2, tiled=True)  9.61 us
    dot_general x2, matrix products, finish_set(): out_rows = jnp.dot(scaled, wd, preferred_element_type=jnp.float32)  9.12 us
  transfers between devices with their start and end apart: 11, of which 6 were waited for; matrix products, arithmetic and copies ran while one was open for 45% of the time, Pallas kernels for 0%

commit v1 on v0

--- a/solution.py
+++ b/solution.py
@@ -1,7 +1,19 @@
+import functools
 import jax
 import jax.numpy as jnp
 from jax import lax
 from jax.sharding import PartitionSpec as P
+
+
+def desk_direct(own_rows, named_axis):
+    v1 = jnp.concatenate(
+        lax.all_to_all(jnp.stack(lax.axis_size(named_axis) * [own_rows], axis=0), named_axis, 0, 0),
+        axis=2,
+    )
+    return v1
+
+
+_register_spots = functools.partial(desk_direct, named_axis="dp")
 
 
 def passed_along(value, axis, steps):
@@ -112,7 +124,7 @@
     scaled, grad_gate, grad_up = hidden_values(gate_val, up_val, back_val, rows_w)
     scaled, grad_gate, grad_up = (
         lax.all_gather(scaled, "dp", axis=2, tiled=True),
-        lax.all_gather(grad_gate, "dp", axis=2, tiled=True),
+        _register_spots(grad_gate),
         lax.all_gather(grad_up, "dp", axis=2, tiled=True),
     )
     own_out, own_in, own_grads = finish_set(

time: 339 us -> 349 us (1.029)
  waiting for transfers between devices: 99.6 us -> 108 us
  local copies, waits for them, and re-layouts: 37.1 us -> 42.4 us
  starting transfers between devices: 15 us -> 9.79 us
  blocking collectives: 0 us -> 5 us
  matrix products: 78 us -> 73.2 us
    ppermute x5, waiting for transfers between devices: 79.7 us -> 108 us  [passed_along(): return lax.ppermute(value, axis, pairs)]
    all_gather x1, waiting for transfers between devices: 9.61 us -> 0.01 us  [per_device(): lax.all_gather(grad_up, 'dp', axis=2, tiled=True)]
    all_gather x1 -> x0, waiting for transfers between devices: 8.07 us -> none  [per_device(): lax.all_gather(grad_gate, 'dp', axis=2, tiled=True)]
    slice x1 -> x4, local copies, waits for them, and re-layouts: 0.07 us -> 6.07 us  [the longest x2 3.71 us: per_device(): grad_gate[1]]
    ppermute x5, starting transfers between devices: 14.8 us -> 9.59 us  [passed_along(): return lax.ppermute(value, axis, pairs)]
    all_to_all x0 -> x1, blocking collectives: none -> 5 us  [desk_direct(): lax.all_to_all(jnp.stack(lax.axis_size(named_axis) * [own_rows], axis=0),...]
  transfers between devices with their start and end apart: 11 -> 10, of which waited for: 6 -> 5; matrix products, arithmetic and copies ran while one was open for 45% -> 40% of each run, Pallas kernels for 0% -> 0%
where the time goes in v1:
time: 349 us; the launch traced here: 344 us
  waiting for transfers between devices  108 us (31%)
  other arithmetic  90.2 us (26%)
  matrix products  73.2 us (21%)
  local copies, waits for them, and re-layouts  42.4 us (12%)
  between operations  14.9 us (4%)
  starting transfers between devices  9.79 us (3%)
  blocking collectives  5 us (1%)
    ppermute x5, waiting for transfers between devices, passed_along(): return lax.ppermute(value, axis, pairs)  108 us
    gather x4, local copies, waits for them, and re-layouts, take_rows(): return jnp.take(array, index, axis=0, mode='fill', fill_value=0)  28.4 us
    scatter-add x2, other arithmetic, per_device(): empty.at[own_index].add(own_in, mode='drop').at[next_index]  24.9 us
    scatter-add x2, other arithmetic, per_device(): empty.at[own_index].add(own_out, mode='drop').at[next_index]  23.3 us
    ppermute x5, starting transfers between devices, passed_along(): return lax.ppermute(value, axis, pairs)  9.59 us
    dot_general x2, matrix products, finish_set(): lax.dot_general(scaled, rows_dy, over_rows, preferred_element_type=jnp.fl...  9.31 us
    dot_general x2, matrix products, finish_set(): lax.dot_general(grad_up, rows_x, over_rows, preferred_element_type=jnp.fl...  9.29 us
    dot_general x2, matrix products, finish_set(): lax.dot_general(grad_gate, rows_x, over_rows, preferred_element_type=jnp....  9.21 us
  transfers between devices with their start and end apart: 10, of which 5 were waited for; matrix products, arithmetic and copies ran while one was open for 40% of the time, Pallas kernels for 0%

profile of v1, /device:TPU:0, one launch (start us, length us, event | category | flops | bytes accessed | tf_op | source)
XLA Modules:
  0.0 343.7 jit_solution(10943472209555040953)
XLA Ops:
  11.9 7.1 %gather_fusion.5 = bf16[512,2048]{1,0:T(8,128)(2,1)} fusion(bf16[512,2048]{1,0:T(8,128)(2,1)} %param.14, s32[1024]{0:T(1024)S(1)} %pad_clamp_fusion), kind=kCustom, calls=%fused_computation.5.clone | custom fusion | bytes 4196352 | tf_op jit(solution)/shard_map/jit(_take)/gather | solution.py:54
  19.0 7.1 %gather_fusion.3 = bf16[512,2048]{1,0:T(8,128)(2,1)} fusion(bf16[512,2048]{1,0:T(8,128)(2,1)} %param.13, s32[1024]{0:T(1024)S(1)} %pad_clamp_fusion), kind=kCustom, calls=%fused_computation.3.clone | custom fusion | bytes 4196352 | tf_op jit(solution)/shard_map/jit(_take)/gather | solution.py:54
  27.4 3.5 %gather_fusion.1 = bf16[512]{0:T(512)(128)(2,1)S(1)} fusion(bf16[512]{0:T(512)(128)(2,1)S(1)} %broadcast_multiply_fusion, s32[1024]{0:T(1024)S(1)} %pad_clamp_fusion), kind=kCustom, calls=%fused_computation.2.clone | custom fusion | bytes 4096 | tf_op jit(solution)/shard_map/jit(_take)/gather | solution.py:41
  30.9 4.6 %broadcast_select_fusion = (bf16[512,2048]{1,0:T(8,128)(2,1)}, bf16[512,2048]{1,0:T(8,128)(2,1)}) fusion(bf16[512,2048]{1,0:T(8,128)(2,1)} %gather_fusion.5, pred[512]{0:T(512)(128)(4,1)S(1)} %get-tuple-element.14, bf16[512,2048]{1,0:T(8,128)(2,1)} %gather_fusion.3), kind=kLoop, calls=%fused_computation.60 | loop fusion | flops 2097152 | bytes 8389120 | tf_op jit(solution)/shard_map/jit(_take)/select_n | solution.py:54
  39.9 7.1 %gather_fusion.2 = bf16[512,2048]{1,0:T(8,128)(2,1)} fusion(bf16[512,2048]{1,0:T(8,128)(2,1)} %param.13, s32[1024]{0:T(1024)S(1)} %pad_clamp_fusion.1), kind=kCustom, calls=%fused_computation.1.clone | custom fusion | bytes 4196352 | tf_op jit(solution)/shard_map/jit(_take)/gather | solution.py:54
  47.0 3.5 %gather_fusion = f32[512]{0:T(512)S(1)} fusion(f32[512]{0:T(512)S(1)} %get-tuple-element.7, s32[1024]{0:T(1024)S(1)} %pad_clamp_fusion.1), kind=kCustom, calls=%fused_computation.clone | custom fusion | bytes 6144 | tf_op jit(solution)/shard_map/jit(_take)/gather | solution.py:41
  53.9 34.7 %collective-permute-done.1 = bf16[512,2048]{1,0:T(8,128)(2,1)} collective-permute-done((bf16[512,2048]{1,0:T(8,128)(2,1)}, bf16[512,2048]{1,0:T(8,128)(2,1)}, u32[]{:S(2)}, u32[]{:S(2)}) %collective-permute-start.1) | collective-permute-done | bytes 2097184 | tf_op jit(solution)/shard_map/ppermute | solution.py:22
  94.0 4.5 %fusion.48 = f32[1,512,768]{2,1,0:T(8,128)S(1)} fusion(bf16[1,768,2048]{2,1,0:T(8,128)(2,1)} %param.20, bf16[512,2048]{1,0:T(8,128)(2,1)} %gather_fusion.2, pred[512]{0:T(512)(128)(4,1)S(1)} %get-tuple-element.12), kind=kOutput, calls=%fused_computation.72 | convolution fusion | flops 1611661312 | bytes 6816256 | tf_op jit(solution)/shard_map/dot_general | solution.py:108
  104.5 7.1 %gather_fusion.4 = bf16[512,2048]{1,0:T(8,128)(2,1)} fusion(bf16[512,2048]{1,0:T(8,128)(2,1)} %param.14, s32[1024]{0:T(1024)S(1)} %pad_clamp_fusion.1), kind=kCustom, calls=%fused_computation.4.clone | custom fusion | bytes 4196352 | tf_op jit(solution)/shard_map/jit(_take)/gather | solution.py:54
  111.6 5.5 %fusion.54 = f32[1,512,768]{2,1,0:T(8,128)S(1)} fusion(bf16[1,768,2048]{2,1,0:T(8,128)(2,1)} %param.21, bf16[512,2048]{1,0:T(8,128)(2,1)} %gather_fusion.4, pred[512]{0:T(512)(128)(4,1)S(1)} %get-tuple-element.12), kind=kOutput, calls=%fused_computation.74 | convolution fusion | flops 1611661312 | bytes 6816256 | tf_op jit(solution)/shard_map/dot_general | solution.py:114
  117.1 38.3 %collective-permute-done.3 = bf16[512,2048]{1,0:T(8,128)(2,1)} collective-permute-done((bf16[512,2048]{1,0:T(8,128)(2,1)}, bf16[512,2048]{1,0:T(8,128)(2,1)}, u32[]{:S(2)}, u32[]{:S(2)}) %collective-permute-start.3) | collective-permute-done | bytes 2097184 | tf_op jit(solution)/shard_map/ppermute | solution.py:22
  160.8 7.2 %collective-permute-done = bf16[512]{0:T(512)(128)(2,1)S(1)} collective-permute-done((bf16[512]{0:T(512)(128)(2,1)S(1)}, bf16[512]{0:T(512)(128)(2,1)S(1)}, u32[]{:S(2)}, u32[]{:S(2)}) %collective-permute-start) | collective-permute-done | bytes 1056 | tf_op jit(solution)/shard_map/ppermute | solution.py:22
  168.1 4.7 %multiply_convert_fusion = (bf16[2,512,384]{2,1,0:T(8,128)(2,1)}, bf16[1,2,512,384]{3,2,1,0:T(8,128)(2,1)}, bf16[2,512,384]{2,1,0:T(8,128)(2,1)}) fusion(f32[2,512,384]{2,1,0:T(8,128)} %reduce-scatter.8.cloned.1.call-done, f32[2,512]{1,0:T(2,128)S(1)} %pad_maximum_fusion.4, f32[2,512,384]{2,1,0:T(8,128)} %reduce-scatter.4.cloned.1.call-done, ...), kind=kLoop, calls=%fused_computation.65 | loop fusion | flops 6684672 | bytes 7081984 | tf_op jit(solution)/shard_map/convert_element_type | solution.py:49
  174.4 5.0 %all_to_all.5 = bf16[2,2,512,384]{3,2,1,0:T(8,128)(2,1)S(1)} all-to-all(bf16[2,2,512,384]{3,2,1,0:T(8,128)(2,1)S(1)} %pad_maximum_fusion.3), channel_id=1, replica_groups=mesh['expert'=16,'dp'=2] {'dp'}, dimensions={0} | all-to-all | bytes 3145728 | tf_op jit(solution)/shard_map/all_to_all | solution.py:10
  185.4 5.4 %convolution_convert_fusion.5 = bf16[768,2048]{1,0:T(8,128)(2,1)} fusion(bf16[512,768]{0,1:T(8,128)(2,1)} %bitcast.108, bf16[512,2048]{1,0:T(8,128)(2,1)} %gather_fusion.2, pred[512]{0:T(512)(128)(4,1)S(1)} %get-tuple-element.12), kind=kOutput, calls=%fused_computation.25 | convolution fusion | flops 1613234176 | bytes 6029824 | tf_op jit(solution)/shard_map/dot_general | solution.py:63
  190.9 3.8 %fusion.27 = f32[512,2048]{1,0:T(8,128)} fusion(bf16[512,768]{0,1:T(8,128)(2,1)S(1)} %bitcast.109, bf16[1,768,2048]{2,1,0:T(8,128)(2,1)S(1)} %copy-done), kind=kOutput, calls=%fused_computation.50 | convolution fusion | flops 1610612736 | bytes 8126464 | tf_op jit(solution)/shard_map/dot_general | solution.py:59
  194.7 3.8 %convolution_convert_fusion.4 = bf16[768,2048]{1,0:T(8,128)(2,1)S(1)} fusion(bf16[512,768]{0,1:T(8,128)(2,1)} %bitcast.110, bf16[512,2048]{1,0:T(8,128)(2,1)} %collective-permute-done.1), kind=kOutput, calls=%fused_computation.24 | convolution fusion | flops 1612185600 | bytes 6029312 | tf_op jit(solution)/shard_map/dot_general | solution.py:63
  201.6 5.7 %convolution_convert_fusion.2 = bf16[768,2048]{1,0:T(8,128)(2,1)} fusion(bf16[512,2048]{1,0:T(8,128)(2,1)} %collective-permute-done.1, bf16[2,512,768]{2,1,0:T(8,128)(2,1)} %all-gather.5.cloned.1.call-done), kind=kOutput, calls=%fused_computation.22 | convolution fusion | flops 1612185600 | bytes 6029312 | tf_op jit(solution)/shard_map/dot_general | solution.py:64
  207.3 3.6 %convolution_convert_fusion.3 = bf16[768,2048]{1,0:T(8,128)(2,1)} fusion(bf16[2,512,768]{2,1,0:T(8,128)(2,1)S(1)} %copy-done.12, bf16[512,2048]{1,0:T(8,128)(2,1)S(1)} %copy-done.5, pred[512]{0:T(512)(128)(4,1)S(1)} %get-tuple-element.12), kind=kOutput, calls=%fused_computation.23 | convolution fusion | flops 1613234176 | bytes 6029824 | tf_op jit(solution)/shard_map/dot_general | solution.py:64
  210.9 5.5 %convolution_convert_fusion = bf16[768,2048]{1,0:T(8,128)(2,1)} fusion(bf16[512,2048]{1,0:T(8,128)(2,1)} %collective-permute-done.3, bf16[2,512,768]{2,1,0:T(8,128)(2,1)} %all-gather.3.cloned.1.call-done), kind=kOutput, calls=%fused_computation.20 | convolution fusion | flops 1612185600 | bytes 6029312 | tf_op jit(solution)/shard_map/dot_general | solution.py:65
  216.4 3.8 %convolution_convert_fusion.1 = bf16[768,2048]{1,0:T(8,128)(2,1)} fusion(bf16[512,2048]{1,0:T(8,128)(2,1)S(1)} %copy-done.6, pred[512]{0:T(512)(128)(4,1)S(1)} %get-tuple-element.12, bf16[2,512,768]{2,1,0:T(8,128)(2,1)S(1)} %copy-done.14), kind=kOutput, calls=%fused_computation.21 | convolution fusion | flops 1613234176 | bytes 6029824 | tf_op jit(solution)/shard_map/dot_general | solution.py:65
  225.3 5.2 %collective-permute-start.4 = (bf16[512,2048]{1,0:T(8,128)(2,1)}, bf16[512,2048]{1,0:T(8,128)(2,1)}, u32[]{:S(2)}, u32[]{:S(2)}) collective-permute-start(bf16[512,2048]{1,0:T(8,128)(2,1)} %add_convert_fusion.3), channel_id=1, source_target_pairs={{0,30},{2,0},{4,2},{6,4},{8,6},{10,8},{12,10},{14,12},{16,14},{18,... | collective-permute-start | bytes 6291464 | tf_op jit(solution)/shard_map/ppermute | solution.py:22
  234.2 3.8 %fusion.15 = f32[512,2048]{1,0:T(8,128)} fusion(bf16[1,768,2048]{2,1,0:T(8,128)(2,1)S(1)} %copy-done.9, bf16[2,512,768]{2,1,0:T(8,128)(2,1)S(1)} %copy-done.14), kind=kOutput, calls=%fused_computation.38 | convolution fusion | flops 1610612736 | bytes 8126464 | tf_op jit(solution)/shard_map/dot_general | solution.py:58
  237.9 11.0 %scatter_custom_fusion = f32[512,2048]{1,0:T(8,128)} fusion(s32[512]{0:T(512)S(1)} %bitcast.118, f32[512,2048]{1,0:T(8,128)} %fusion.15, f32[]{:T(128)} %constant.31.clone.1), kind=kCustom, calls=%fused_computation.58 | custom fusion | flops 1048576 | bytes 4194816 | tf_op jit(solution)/shard_map/scatter-add | solution.py:165
  249.0 5.9 %fusion.19 = f32[512,2048]{1,0:T(8,128)} fusion(bf16[1,768,2048]{2,1,0:T(8,128)(2,1)} %param.20, bf16[2,512,768]{2,1,0:T(8,128)(2,1)} %all-gather.5.cloned.1.call-done), kind=kOutput, calls=%fused_computation.42 | convolution fusion | flops 1610612736 | bytes 8126464 | tf_op jit(solution)/shard_map/dot_general | solution.py:60
  254.9 12.5 %scatter_custom_fusion.2 = f32[512,2048]{1,0:T(8,128)} fusion(s32[512]{0:T(512)S(1)} %bitcast.119, f32[512,2048]{1,0:T(8,128)} %fusion.27, f32[512,2048]{1,0:T(8,128)} %fusion.19, f32[]{:T(128)} %constant.31.clone.1), kind=kCustom, calls=%fused_computation.16 | custom fusion | flops 2097152 | bytes 12582916 | tf_op jit(solution)/shard_map/scatter-add | solution.py:167
  267.4 6.2 %fusion.7 = bf16[1,768,2048]{2,1,0:T(8,128)(2,1)} fusion(bf16[768,2048]{1,0:T(8,128)(2,1)} %convolution_convert_fusion.2, bf16[768,2048]{1,0:T(8,128)(2,1)} %convolution_convert_fusion.3), kind=kLoop, calls=%fused_computation.27 | loop fusion | flops 6291456 | bytes 9437184 | tf_op jit(solution)/shard_map/broadcast_in_dim | solution.py:172
  276.8 12.4 %scatter_custom_fusion.3 = f32[512,2048]{1,0:T(8,128)} fusion(f32[512,2048]{1,0:T(8,128)} %scatter_custom_fusion.2, s32[512]{0:T(512)S(1)} %bitcast.116, bf16[512,2048]{1,0:T(8,128)(2,1)} %collective-permute-done.4), kind=kCustom, calls=%fused_computation.13 | custom fusion | flops 2097152 | bytes 6291456 | tf_op jit(solution)/shard_map/scatter-add | solution.py:167
  289.3 3.8 %convert_element_type.116 = bf16[512,2048]{1,0:T(8,128)(2,1)} convert(f32[512,2048]{1,0:T(8,128)} %scatter_custom_fusion.3) | non-fusion elementwise | flops 1048576 | bytes 6291456 | tf_op jit(solution)/shard_map/convert_element_type | solution.py:170
  293.1 27.8 %collective-permute-done.2 = bf16[512,2048]{1,0:T(8,128)(2,1)} collective-permute-done((bf16[512,2048]{1,0:T(8,128)(2,1)}, bf16[512,2048]{1,0:T(8,128)(2,1)}, u32[]{:S(2)}, u32[]{:S(2)}) %collective-permute-start.2) | collective-permute-done | bytes 2097184 | tf_op jit(solution)/shard_map/ppermute | solution.py:22
  320.9 12.2 %scatter_custom_fusion.1 = f32[512,2048]{1,0:T(8,128)} fusion(f32[512,2048]{1,0:T(8,128)} %scatter_custom_fusion, s32[512]{0:T(512)S(1)} %bitcast.117, bf16[512,2048]{1,0:T(8,128)(2,1)} %collective-permute-done.2), kind=kCustom, calls=%fused_computation.18 | custom fusion | flops 2097152 | bytes 6291456 | tf_op jit(solution)/shard_map/scatter-add | solution.py:165
  333.2 3.8 %convert_element_type.111 = bf16[512,2048]{1,0:T(8,128)(2,1)} convert(f32[512,2048]{1,0:T(8,128)} %scatter_custom_fusion.1) | non-fusion elementwise | flops 1048576 | bytes 6291456 | tf_op jit(solution)/shard_map/convert_element_type | solution.py:169
  (100 shorter events, 52.7 us)
Async XLA Ops:
  7.2 43.3 %copy-start = (bf16[1,768,2048]{2,1,0:T(8,128)(2,1)S(1)}, bf16[1,768,2048]{2,1,0:T(8,128)(2,1)}, u32[]{:S(2)}) copy-start(bf16[1,768,2048]{2,1,0:T(8,128)(2,1)} %param.19) | copy-start | bytes 9437188
  7.2 160.8 %reduce-scatter.4.cloned.1.call-start = ((), (), s32[]{:S(2)}) async-start(), calls=%async_computation.4 | async-start | bytes 4718592 | tf_op jit(solution)/shard_map/reduce_scatter | solution.py:119
  19.0 7.1 %copy-start.15 = (s32[16]{0:T(128)S(1)}, s32[16]{0:T(128)}, u32[]{:S(2)}) copy-start(s32[16]{0:T(128)} %param.18) | copy-start | bytes 196
  35.5 53.2 %collective-permute-start.1 = (bf16[512,2048]{1,0:T(8,128)(2,1)}, bf16[512,2048]{1,0:T(8,128)(2,1)}, u32[]{:S(2)}, u32[]{:S(2)}) collective-permute-start(bf16[512,2048]{1,0:T(8,128)(2,1)} %get-tuple-element.27), channel_id=1, source_target_pairs={{0,2},{2,4},{4,6},{6,8},{8,10},{10,12},{12,14},{14,16},{16,18},{18... | collective-permute-start | bytes 6291464 | tf_op jit(solution)/shard_map/ppermute | solution.py:22
  94.0 74.1 %reduce-scatter.6.cloned.1.call-start = ((), (), s32[]{:S(2)}) async-start(), calls=%async_computation.5 | async-start | bytes 4718592 | tf_op jit(solution)/shard_map/reduce_scatter | solution.py:120
  94.0 4.5 %copy-start.10 = (bf16[1,768,2048]{2,1,0:T(8,128)(2,1)S(1)}, bf16[1,768,2048]{2,1,0:T(8,128)(2,1)}, u32[]{:S(2)}) copy-start(bf16[1,768,2048]{2,1,0:T(8,128)(2,1)} %param.20) | copy-start | bytes 9437188
  103.9 64.2 %reduce-scatter.8.cloned.1.call-start = ((), (), s32[]{:S(2)}) async-start(), calls=%async_computation.7 | async-start | bytes 4718592 | tf_op jit(solution)/shard_map/reduce_scatter | solution.py:121
  103.9 51.4 %collective-permute-start.3 = (bf16[512,2048]{1,0:T(8,128)(2,1)}, bf16[512,2048]{1,0:T(8,128)(2,1)}, u32[]{:S(2)}, u32[]{:S(2)}) collective-permute-start(bf16[512,2048]{1,0:T(8,128)(2,1)} %get-tuple-element.26), channel_id=1, source_target_pairs={{0,2},{2,4},{4,6},{6,8},{8,10},{10,12},{12,14},{14,16},{16,18},{18... | collective-permute-start | bytes 6291464 | tf_op jit(solution)/shard_map/ppermute | solution.py:22
  111.6 43.7 %copy-start.8 = (bf16[1,768,2048]{2,1,0:T(8,128)(2,1)S(1)}, bf16[1,768,2048]{2,1,0:T(8,128)(2,1)}, u32[]{:S(2)}) copy-start(bf16[1,768,2048]{2,1,0:T(8,128)(2,1)} %param.21) | copy-start | bytes 9437188
  160.7 40.9 %all-gather.5.cloned.1.call-start = ((), (), s32[]{:S(2)}) async-start(), calls=%async_computation.8 | async-start | bytes 2359296 | tf_op jit(solution)/shard_map/all_gather | solution.py:128
  160.7 7.2 %collective-permute-start = (bf16[512]{0:T(512)(128)(2,1)S(1)}, bf16[512]{0:T(512)(128)(2,1)S(1)}, u32[]{:S(2)}, u32[]{:S(2)}) collective-permute-start(bf16[512]{0:T(512)(128)(2,1)S(1)} %get-tuple-element.13), channel_id=1, source_target_pairs={{0,2},{2,4},{4,6},{6,8},{8,10},{10,12},{12,14},{14,16},{16,18},{18... | collective-permute-start | bytes 3080 | tf_op jit(solution)/shard_map/ppermute | solution.py:22
  172.8 38.1 %all-gather.3.cloned.1.call-start = ((), (), s32[]{:S(2)}) async-start(), calls=%async_computation.6 | async-start | bytes 2359296 | tf_op jit(solution)/shard_map/all_gather | solution.py:126
  185.4 5.4 %copy-start.1 = (bf16[1,512,2,384]{1,3,2,0:T(8,128)(2,1)S(1)}, bf16[1,512,2,384]{1,3,2,0:T(8,128)(2,1)}, u32[]{:S(2)}) copy-start(bf16[1,512,2,384]{1,3,2,0:T(8,128)(2,1)} %copy.16) | copy-start | bytes 2359300
  194.7 3.8 %copy-start.4 = (bf16[768,2048]{1,0:T(8,128)(2,1)S(1)}, bf16[768,2048]{1,0:T(8,128)(2,1)}, u32[]{:S(2)}) copy-start(bf16[768,2048]{1,0:T(8,128)(2,1)} %convolution_convert_fusion.5) | copy-start | bytes 9437188
  201.6 5.7 %copy-start.5 = (bf16[512,2048]{1,0:T(8,128)(2,1)S(1)}, bf16[512,2048]{1,0:T(8,128)(2,1)}, u32[]{:S(2)}) copy-start(bf16[512,2048]{1,0:T(8,128)(2,1)} %gather_fusion.2) | copy-start | bytes 6291460
  201.6 5.7 %copy-start.12 = (bf16[2,512,768]{2,1,0:T(8,128)(2,1)S(1)}, bf16[2,512,768]{2,1,0:T(8,128)(2,1)}, u32[]{:S(2)}) copy-start(bf16[2,512,768]{2,1,0:T(8,128)(2,1)} %all-gather.5.cloned.1.call-done) | copy-start | bytes 4718596
  210.9 5.5 %copy-start.6 = (bf16[512,2048]{1,0:T(8,128)(2,1)S(1)}, bf16[512,2048]{1,0:T(8,128)(2,1)}, u32[]{:S(2)}) copy-start(bf16[512,2048]{1,0:T(8,128)(2,1)} %gather_fusion.4) | copy-start | bytes 6291460
  210.9 5.5 %copy-start.14 = (bf16[2,512,768]{2,1,0:T(8,128)(2,1)S(1)}, bf16[2,512,768]{2,1,0:T(8,128)(2,1)}, u32[]{:S(2)}) copy-start(bf16[2,512,768]{2,1,0:T(8,128)(2,1)} %all-gather.3.cloned.1.call-done) | copy-start | bytes 4718596
  216.3 3.9 %copy-start.11 = (bf16[1,768,2048]{2,1,0:T(8,128)(2,1)S(1)}, bf16[1,768,2048]{2,1,0:T(8,128)(2,1)}, u32[]{:S(2)}) copy-start(bf16[1,768,2048]{2,1,0:T(8,128)(2,1)} %param.20) | copy-start | bytes 9437188
  216.4 3.9 %copy-start.13 = (bf16[2,512,768]{2,1,0:T(8,128)(2,1)S(1)}, bf16[2,512,768]{2,1,0:T(8,128)(2,1)}, u32[]{:S(2)}) copy-start(bf16[2,512,768]{2,1,0:T(8,128)(2,1)} %all-gather.5.cloned.1.call-done) | copy-start | bytes 4718596
  220.2 1.8 copy-start.7
  222.0 8.5 %copy-start.9 = (bf16[1,768,2048]{2,1,0:T(8,128)(2,1)S(1)}, bf16[1,768,2048]{2,1,0:T(8,128)(2,1)}, u32[]{:S(2)}) copy-start(bf16[1,768,2048]{2,1,0:T(8,128)(2,1)} %param.21) | copy-start | bytes 9437188
  225.3 51.5 %collective-permute-start.4 = (bf16[512,2048]{1,0:T(8,128)(2,1)}, bf16[512,2048]{1,0:T(8,128)(2,1)}, u32[]{:S(2)}, u32[]{:S(2)}) collective-permute-start(bf16[512,2048]{1,0:T(8,128)(2,1)} %add_convert_fusion.3), channel_id=1, source_target_pairs={{0,30},{2,0},{4,2},{6,4},{8,6},{10,8},{12,10},{14,12},{16,14},{18,... | collective-permute-start | bytes 6291464 | tf_op jit(solution)/shard_map/ppermute | solution.py:22
  233.6 87.3 %collective-permute-start.2 = (bf16[512,2048]{1,0:T(8,128)(2,1)}, bf16[512,2048]{1,0:T(8,128)(2,1)}, u32[]{:S(2)}, u32[]{:S(2)}) collective-permute-start(bf16[512,2048]{1,0:T(8,128)(2,1)} %fusion.33), channel_id=1, source_target_pairs={{0,30},{2,0},{4,2},{6,4},{8,6},{10,8},{12,10},{14,12},{16,14},{18,... | collective-permute-start | bytes 6291464 | tf_op jit(solution)/shard_map/ppermute | solution.py:22
  267.4 6.2 %copy-start.2 = (bf16[768,2048]{1,0:T(8,128)(2,1)S(1)}, bf16[768,2048]{1,0:T(8,128)(2,1)}, u32[]{:S(2)}) copy-start(bf16[768,2048]{1,0:T(8,128)(2,1)} %convolution_convert_fusion) | copy-start | bytes 9437188
  267.4 6.2 %copy-start.3 = (bf16[768,2048]{1,0:T(8,128)(2,1)S(1)}, bf16[768,2048]{1,0:T(8,128)(2,1)}, u32[]{:S(2)}) copy-start(bf16[768,2048]{1,0:T(8,128)(2,1)} %convolution_convert_fusion.1) | copy-start | bytes 9437188
Sparse Core Ops, SparseCore 0:
  94.1 8.4 reduce-scatter.3
  105.4 12.2 reduce-scatter.5
  160.8 6.8 reduce-scatter.7
  172.9 10.6 all-gather.4
  194.8 10.6 all-gather.2
